TPU v7x, 32 devices: a 4x4x1 block of a 4x4x8 slice. The times are simulated.
32 devices in a mesh: data: 1 (over z), row: 4 (over y), col: 4 (over x), core: 2 (over core).
Axes of the slice: x: 4, y: 4, z: 1, core: 2. Of those that a mesh axis runs over, the one named last changes fastest.
The devices are a block of a 4x4x8 slice.
Arguments:
- tokens: bfloat16 [2, 2048, 2048], P('data', ('row', 'col', 'core'))
- w_qkv: bfloat16 [2048, 3, 32, 64], replicated
- w_out: bfloat16 [32, 64, 2048], replicated
Outputs:
- output: bfloat16 [2, 2048, 2048], P('data', ('row', 'col', 'core'))
All inputs are finite; a program needn't handle non-finite values.
Results may differ from a plain program's by a relative error of at most 0.00748467.
Values are sent between devices in bfloat16 or wider.
A program may use at most 768 MiB of HBM per device.

v0:
```python
import jax
import jax.numpy as jnp
from jax import lax
from jax.sharding import PartitionSpec as P


def init_state(queries):
    batch_n, query_n, head_n, head_dim = queries.shape
    run_max = jnp.full((batch_n, head_n, query_n), -jnp.inf, jnp.float32)
    run_acc = jnp.zeros((batch_n, head_n, query_n, head_dim), jnp.float32)
    return run_max, jnp.zeros_like(run_max), run_acc


def attend_keys(queries, kv_rows, state):
    blk_len = min(128, kv_rows.shape[1])
    logit_scale = queries.shape[-1] ** -0.5

    def key_step(blk_index, run_state):
        run_max, run_sum, run_acc = run_state
        kv_piece = lax.dynamic_slice_in_dim(kv_rows, blk_index * blk_len, blk_len, axis=1)
        scores = jnp.einsum("bqhd,bkhd->bhqk", queries, kv_piece[:, :, 0], preferred_element_type=jnp.float32) * logit_scale
        new_max = jnp.maximum(run_max, jnp.max(scores, axis=-1))
        rescale = jnp.exp(run_max - new_max)
        weights = jnp.exp(scores - new_max[..., None])
        run_sum = run_sum * rescale + jnp.sum(weights, axis=-1)
        run_acc = run_acc * rescale[..., None] + jnp.einsum("bhqk,bkhd->bhqd", weights.astype(jnp.bfloat16), kv_piece[:, :, 1], preferred_element_type=jnp.float32)
        return new_max, run_sum, run_acc

    return lax.fori_loop(0, kv_rows.shape[1] // blk_len, key_step, state)


def finish_state(state):
    run_sum = state[1]
    run_acc = state[2]
    attn_out = (run_acc / run_sum[..., None]).astype(jnp.bfloat16)
    return jnp.transpose(attn_out, (0, 2, 1, 3))


def solution(mesh):
    head_axes = ("col", "core")
    tok_spec = P("data", ("row", "col", "core"), None)

    def per_device(tokens, w_qkv, w_out):
        qkv_loc = jnp.einsum("btc,cjhd->btjhd", tokens, w_qkv, preferred_element_type=jnp.float32).astype(jnp.bfloat16)
        qkv_grp = lax.all_to_all(qkv_loc, head_axes, 3, 1, tiled=True)
        queries = qkv_grp[:, :, 0]
        kv_all = lax.all_gather(qkv_grp[:, :, 1:], "row", axis=1, tiled=True)
        attn_out = finish_state(attend_keys(queries, kv_all, init_state(queries)))
        attn_loc = lax.all_to_all(attn_out, head_axes, 1, 2, tiled=True)
        return jnp.einsum("bthd,hdc->btc", attn_loc, w_out, preferred_element_type=jnp.float32).astype(jnp.bfloat16)

    return jax.shard_map(per_device, mesh=mesh, in_specs=(tok_spec, P(), P()), out_specs=tok_spec, check_vma=False)
```

profile of v0, /device:TPU:97, one launch (start us, length us, event | category | flops | bytes accessed | tf_op | source)
XLA Modules:
  0.0 211.9 jit_solution(334697870006147307)
XLA Ops:
  6.6 1.0 copy-done
  7.6 18.1 %fusion.21 = bf16[2,64,3,32,64]{4,1,3,2,0:T(8,128)(2,1)} fusion(bf16[2048,3,32,64]{0,3,2,1:T(8,128)(2,1)} %param.6, bf16[2,64,2048]{2,1,0:T(8,128)(2,1)S(1)} %copy-done), kind=kOutput, calls=%fused_computation.25 | convolution fusion | flops 3222011904 | bytes 27262976 | tf_op jit(solution)/shard_map/btc,cjhd->btjhd/dot_general | solution.py:44
  25.7 4.6 %copy.22 = bf16[2,64,3,32,64]{4,1,2,0,3:T(8,128)(2,1)} copy(bf16[2,64,3,32,64]{4,1,3,2,0:T(8,128)(2,1)} %fusion.21) | data formatting | bytes 3145728 | tf_op jit(solution)/shard_map/convert_element_type | solution.py:44
  30.3 5.8 %reshape.7 = bf16[8,2,49152]{2,1,0:T(2,128)(2,1)S(1)} reshape(bf16[32,2,3,64,64]{4,3,2,1,0:T(8,128)(2,1)} %bitcast.75) | data formatting | bytes 3145728
  36.1 26.4 %all_to_all.36 = bf16[8,2,49152]{2,1,0:T(2,128)(2,1)} all-to-all(bf16[8,2,49152]{2,1,0:T(2,128)(2,1)S(1)} %reshape.7), channel_id=1, replica_groups=mesh['data'=1,'row'=4,'col'=4,'core'=2] {'col','core'}, dimensions={0} | all-to-all | bytes 3145728 | tf_op jit(solution)/shard_map/all_to_all | solution.py:45
  62.4 6.8 %reshape.8 = bf16[32,2,3,64,64]{4,3,2,1,0:T(8,128)(2,1)} reshape(bf16[8,2,49152]{2,1,0:T(2,128)(2,1)} %all_to_all.36) | data formatting | bytes 3145728
  69.2 4.9 %copy.15 = bf16[2,8,64,3,4,64]{2,1,5,4,0,3:T(8,128)(2,1)} copy(bf16[2,8,64,3,4,64]{5,2,3,0,4,1:T(8,128)(2,1)} %bitcast.76) | data formatting | bytes 3145728 | tf_op jit(solution)/shard_map/all_to_all | solution.py:45
  74.1 4.5 %all_to_all.29 = bf16[2,512,3,4,64]{1,4,3,0,2:T(8,128)(2,1)S(1)} reshape(bf16[2,8,64,3,4,64]{2,1,5,4,0,3:T(8,128)(2,1)} %copy.15) | data formatting | bytes 3145728 | tf_op jit(solution)/shard_map/all_to_all | solution.py:45
  78.6 1.2 slice.24
  80.1 1.1 slice_bitcast_fusion
  81.2 45.6 %all-gather.2.cloned.1.call-done = bf16[2,2048,2,4,64]{1,4,3,0,2:T(8,128)(2,1)} async-done(((bf16[2,512,2,4,64]{1,4,3,0,2:T(8,128)(2,1)}), bf16[2,2048,2,4,64]{1,4,3,0,2:T(8,128)(2,1)}) %all-gather.2.cloned.1.call-update) | async-done | bytes 4194320 | tf_op jit(solution)/shard_map/all_gather | solution.py:47
  126.8 55.9 %while.18 = (s32[]{:T(128)}, f32[2,4,512]{2,1,0:T(4,128)S(1)}, f32[2,4,512]{2,1,0:T(4,128)S(1)}, f32[2,4,512,64]{2,3,1,0:T(8,128)S(1)}, bf16[2,2048,2,4,64]{1,4,...) while((s32[]{:T(128)}, f32[2,4,512]{2,1,0:T(4,128)S(1)}, ...), condition=%wide.region_3.0_spmd.clone, body=%wide.region_0.0_spmd.clone.sunk | while | flops 139218944 | bytes 9437383 | solution.py:29
  126.8 1.4 bitcast_reduce_fusion.2
  128.2 0.4 fusion.34
  128.6 1.6 convolution_add_fusion.2
  130.3 1.4 bitcast_reduce_fusion.2
  131.7 0.4 fusion.34
  132.1 1.6 convolution_add_fusion.2
  133.8 1.4 bitcast_reduce_fusion.2
  135.2 0.4 fusion.34
  135.6 1.6 convolution_add_fusion.2
  137.3 1.4 bitcast_reduce_fusion.2
  138.7 0.4 fusion.34
  139.1 1.6 convolution_add_fusion.2
  140.8 1.4 bitcast_reduce_fusion.2
  142.2 0.4 fusion.34
  142.6 1.6 convolution_add_fusion.2
  144.3 1.4 bitcast_reduce_fusion.2
  145.7 0.4 fusion.34
  146.1 1.6 convolution_add_fusion.2
  147.7 1.4 bitcast_reduce_fusion.2
  149.2 0.4 fusion.34
  149.6 1.6 convolution_add_fusion.2
  151.2 1.4 bitcast_reduce_fusion.2
  152.7 0.4 fusion.34
  153.1 1.6 convolution_add_fusion.2
  154.7 1.4 bitcast_reduce_fusion.2
  156.2 0.4 fusion.34
  156.6 1.6 convolution_add_fusion.2
  158.2 1.4 bitcast_reduce_fusion.2
  159.7 0.4 fusion.34
  160.1 1.6 convolution_add_fusion.2
  161.7 1.4 bitcast_reduce_fusion.2
  163.2 0.4 fusion.34
  163.6 1.6 convolution_add_fusion.2
  165.2 1.4 bitcast_reduce_fusion.2
  166.7 0.4 fusion.34
  167.1 1.6 convolution_add_fusion.2
  168.7 1.4 bitcast_reduce_fusion.2
  170.2 0.4 fusion.34
  170.6 1.6 convolution_add_fusion.2
  172.2 1.4 bitcast_reduce_fusion.2
  173.7 0.4 fusion.34
  174.1 1.6 convolution_add_fusion.2
  175.7 1.4 bitcast_reduce_fusion.2
  177.2 0.4 fusion.34
  177.6 1.6 convolution_add_fusion.2
  179.2 1.4 bitcast_reduce_fusion.2
  181.1 1.6 convolution_add_fusion.2
  182.8 0.7 copy.16
  183.6 0.7 reshape.9
  184.3 14.3 %all_to_all.37 = bf16[8,2,16384]{2,1,0:T(2,128)(2,1)S(1)} all-to-all(bf16[8,2,16384]{2,1,0:T(2,128)(2,1)S(1)} %reshape.9), channel_id=1, replica_groups=mesh['data'=1,'row'=4,'col'=4,'core'=2] {'col','core'}, dimensions={0} | all-to-all | bytes 1048576 | tf_op jit(solution)/shard_map/all_to_all | solution.py:49
  198.6 0.7 reshape.10
  199.5 5.5 %fusion.18 = bf16[2,64,2048]{2,1,0:T(8,128)(2,1)} fusion(bf16[2,64,32,64]{3,1,2,0:T(8,128)(2,1)S(1)} %bitcast.79, bf16[32,64,2048]{2,1,0:T(8,128)(2,1)} %param.7), kind=kOutput, calls=%fused_computation.24 | convolution fusion | flops 1074003968 | bytes 9437184 | tf_op jit(solution)/shard_map/bthd,hdc->btc/dot_general | solution.py:50
  (59 shorter events, 1.7 us)
Async XLA Ops:
  6.5 1.0 copy-start
  6.6 120.2 %all-gather.2.cloned.1.call-start = ((), (), s32[]{:S(2)}) async-start(), calls=%async_computation.2 | async-start | bytes 5242880 | tf_op jit(solution)/shard_map/all_gather | solution.py:47
  78.6 1.5 copy-start.1
Sparse Core Ops, SparseCore 0:
  79.9 46.7 all-gather.1
where the time goes:
time: 213 us; the launch traced here: 212 us
  matrix products  72 us (34%)
  waiting for transfers between devices  45.6 us (21%)
  blocking collectives  40.7 us (19%)
  local copies, waits for them, and re-layouts  32.4 us (15%)
  between operations  13.5 us (6%)
  other arithmetic  6.82 us (3%)
    all_gather x1, waiting for transfers between devices, per_device(): kv_all = lax.all_gather(qkv_grp[:, :, 1:], 'row', axis=1, tiled=True)  45.6 us
    all_to_all x1, blocking collectives, per_device(): qkv_grp = lax.all_to_all(qkv_loc, head_axes, 3, 1, tiled=True)  26.4 us
    dot_general x16, matrix products, key_step(): jnp.einsum('bhqk,bkhd->bhqd', weights.astype(jnp.bfloat16), kv_piece[:, :...  25.8 us
    dot_general x16, matrix products, key_step(): jnp.einsum('bqhd,bkhd->bhqk', queries, kv_piece[:, :, 0], preferred_eleme...  22.5 us
    dot_general x1, matrix products, per_device(): jnp.einsum('btc,cjhd->btjhd', tokens, w_qkv, preferred_element_type=jnp.f...  18.1 us
    unnamed x8, local copies, waits for them, and re-layouts  15.2 us
    all_to_all x1, blocking collectives, per_device(): attn_loc = lax.all_to_all(attn_out, head_axes, 1, 2, tiled=True)  14.3 us
    all_to_all x2, local copies, waits for them, and re-layouts, per_device(): qkv_grp = lax.all_to_all(qkv_loc, head_axes, 3, 1, tiled=True)  9.37 us
  transfers between devices with their start and end apart: 1, of which 1 were waited for; matrix products, arithmetic and copies ran while one was open for 1% of the time, Pallas kernels for 0%

commit v1 on v0

v1 whole, which is shorter than its diff:
```python
import functools

import jax
import jax.numpy as jnp
from jax import lax
from jax.experimental import pallas as pl
from jax.experimental.pallas import tpu as pltpu
from jax.sharding import PartitionSpec as P

MESH = pl.DeviceIdType.MESH
F32 = jnp.float32
BF16 = jnp.bfloat16
NT = (((1,), (1,)), ((), ()))
NN = (((1,), (0,)), ((), ()))


def hop_order(rows, cols):
    def hops(d, n):
        return min(d, n - d)

    offs = [(dy, dx) for dy in range(rows) for dx in range(cols)][1:]
    return sorted(offs, key=lambda o: (-hops(o[0], rows) - hops(o[1], cols), hops(o[0], rows), hops(o[1], cols)))


def pack_table(values, base):
    words = []
    for start in range(0, len(values), 8):
        words.append(sum(v * base**i for i, v in enumerate(values[start : start + 8])))
    return words


def kernel(dims, x_ref, wt_ref, wo_ref, y_ref, wbuf, wobuf, sbuf, kv_all, q_all, vt, s0, s1, obuf, ob,
           w_sem, wo_sem, send_sem, recv_sem, osend_sem, orecv_sem):
    rows, cols, tok, pair, head = dims
    chips = rows * cols
    ch = x_ref.shape[1]
    z = lax.axis_index("data")
    r = lax.axis_index("row")
    c = lax.axis_index("col")
    k = lax.axis_index("core")
    my_chip = r * cols + c
    me = my_chip * 2 + k
    order = hop_order(rows, cols)
    n_step = len(order)
    dy_words = pack_table([o[0] for o in order], rows)
    dx_words = pack_table([o[1] for o in order], cols)

    def digit(words, base, i):
        val = words[0]
        for w, word in enumerate(words[1:]):
            val = val + (word - words[w]) * (jnp.minimum(i // (8 * (w + 1)), 1))
        shift = base.bit_length() - 1
        return lax.rem(lax.shift_right_logical(jnp.int32(0) + val, shift * lax.rem(i, 8)), base)

    def step_offset(i):
        if isinstance(i, int):
            return order[i]
        return digit(dy_words, rows, i), digit(dx_words, cols, i)

    def chip_to(i):
        dy, dx = step_offset(i)
        rr, cc = lax.rem(r + dy, rows), lax.rem(c + dx, cols)
        return rr, cc, rr * cols + cc

    def chip_from(i):
        dy, dx = step_offset(i)
        rr, cc = lax.rem(r + rows - dy, rows), lax.rem(c + cols - dx, cols)
        return rr, cc, rr * cols + cc

    def w_copy(slot, j, chip):
        return pltpu.make_async_copy(
            wt_ref.at[pl.ds(pl.multiple_of((j * chips + chip) * pair, pair), pair)],
            wbuf.at[slot, j], w_sem.at[j, slot])

    for j in (1, 2, 0):
        w_copy(0, j, my_chip).start()
    for i in range(n_step):
        chip = chip_to(i)[2]
        w_copy(i + 1, 1, chip).start()
        w_copy(i + 1, 2, chip).start()

    barrier = pltpu.get_barrier_semaphore()
    for i in range(n_step):
        rr, cc, _ = chip_to(i)
        for core in range(2):
            pl.semaphore_signal(barrier, inc=1, device_id=(z, rr, cc, core), device_id_type=MESH)
    pl.semaphore_signal(barrier, inc=1, device_id=(z, r, c, 1 - k), device_id_type=MESH)
    for i in range(n_step):
        w_copy(i + 1, 0, chip_to(i)[2]).start()
    wo_copy = pltpu.make_async_copy(wo_ref, wobuf, wo_sem)
    wo_copy.start()

    def project(slot, j):
        return lax.dot_general(x_ref[...], wbuf[slot, j], NT, preferred_element_type=F32).astype(BF16)

    def keep(slot, j, piece):
        val = project(slot, j)
        for b in range(2):
            sbuf[slot, b, piece] = val[b * tok:(b + 1) * tok]

    def kv_send(slot, b, rr, cc):
        return pltpu.make_async_remote_copy(
            src_ref=sbuf.at[slot, b, pl.ds(0, 2)], dst_ref=kv_all.at[:, me],
            send_sem=send_sem.at[0, slot, b], recv_sem=recv_sem.at[0, me],
            device_id=(z, rr, cc, b), device_id_type=MESH)

    def q_send(slot, b, rr, cc):
        return pltpu.make_async_remote_copy(
            src_ref=sbuf.at[slot, b, 2], dst_ref=q_all.at[me],
            send_sem=send_sem.at[1, slot, b], recv_sem=recv_sem.at[1, me],
            device_id=(z, rr, cc, b), device_id_type=MESH)

    def kv_wait(dev):
        pltpu.make_async_remote_copy(
            src_ref=sbuf.at[0, 0, pl.ds(0, 2)], dst_ref=kv_all.at[:, dev],
            send_sem=send_sem.at[0, 0, 0], recv_sem=recv_sem.at[0, dev],
            device_id=(z, r, c, k), device_id_type=MESH).wait_recv()

    def q_wait(dev):
        pltpu.make_async_remote_copy(
            src_ref=sbuf.at[0, 0, 2], dst_ref=q_all.at[dev],
            send_sem=send_sem.at[1, 0, 0], recv_sem=recv_sem.at[1, dev],
            device_id=(z, r, c, k), device_id_type=MESH).wait_recv()

    for j, piece in ((1, 0), (2, 1), (0, 2)):
        w_copy(0, j, my_chip).wait()
        keep(0, j, piece)
    for piece in range(2):
        kv_all[piece, me] = sbuf[0, k, piece]
    q_all[me] = sbuf[0, k, 2]

    pl.semaphore_wait(barrier, 2 * n_step + 1)
    kv_send(0, 1 - k, r, c).start()
    q_send(0, 1 - k, r, c).start()

    def kv_step(i, _):
        rr, cc, chip = chip_to(i)
        for j, piece in ((1, 0), (2, 1)):
            w_copy(i + 1, j, chip).wait()
            keep(i + 1, j, piece)
        for b in range(2):
            kv_send(i + 1, b, rr, cc).start()
        return 0

    def q_step(i, _):
        rr, cc, chip = chip_to(i)
        w_copy(i + 1, 0, chip).wait()
        keep(i + 1, 0, 2)
        for b in range(2):
            q_send(i + 1, b, rr, cc).start()
        return 0

    lax.fori_loop(0, n_step, kv_step, 0)
    lax.fori_loop(0, n_step, q_step, 0)

    def flip(chip):
        val = kv_all[1, pl.ds(2 * chip, 2)].reshape(2 * tok, pair)
        vt[:, pl.ds(pl.multiple_of(chip * 2 * tok, 2 * tok), 2 * tok)] = val.T

    def kv_arrive(i, _):
        _, _, chip = chip_from(i)
        kv_wait(2 * chip)
        kv_wait(2 * chip + 1)
        flip(chip)
        return 0

    lax.fori_loop(0, n_step, kv_arrive, 0)
    kv_wait(2 * my_chip + 1 - k)
    flip(my_chip)

    keys = kv_all.shape[1] * tok
    chunk = 4 * 2 * tok
    n_chunk = keys // chunk
    lanes = 2 * 2 * tok

    def queries(chip):
        q = q_all[pl.ds(2 * chip, 2)].reshape(2 * tok, pair) * BF16(head**-0.5)
        lane = lax.broadcasted_iota(jnp.int32, q.shape, 1)
        first = lane < head
        zero = jnp.zeros_like(q)
        return jnp.concatenate([jnp.where(first, q, zero), jnp.where(first, zero, q)], axis=0)

    def scores(qq, scr, ci):
        keys_c = kv_all[0, pl.ds(ci * (chunk // tok), chunk // tok)].reshape(chunk, pair)
        s = lax.dot_general(keys_c, qq, NT, preferred_element_type=F32)
        scr[pl.ds(ci * chunk, chunk)] = s
        return jnp.max(s.reshape(chunk // 8, 8, lanes), axis=0)

    def all_scores(chip, scr):
        qq = queries(chip)
        top = scores(qq, scr, 0)
        for ci in range(1, n_chunk):
            top = jnp.maximum(top, scores(qq, scr, ci))
        return jnp.max(top, axis=0, keepdims=True)

    def finish(chip, scr, top):
        total = jnp.zeros((8, lanes), F32)
        acc = jnp.zeros((pair, lanes), F32)
        for ci in range(n_chunk):
            w = jnp.exp(scr[pl.ds(ci * chunk, chunk)] - top)
            total += jnp.sum(w.reshape(chunk // 8, 8, lanes), axis=0)
            acc += lax.dot_general(vt[:, ci * chunk:(ci + 1) * chunk], w.astype(BF16), NN, preferred_element_type=F32)
        total = jnp.sum(total, axis=0, keepdims=True)
        half = lanes // 2
        out = jnp.concatenate([acc[:head, :half] / total[:, :half], acc[head:, half:] / total[:, half:]], axis=0)
        return out.T.astype(BF16)

    def o_send(slot, core, rr, cc):
        return pltpu.make_async_remote_copy(
            src_ref=obuf.at[slot, core],
            dst_ref=ob.at[k, :, pl.ds(pl.multiple_of(my_chip * pair, pair), pair)],
            send_sem=osend_sem.at[slot, core], recv_sem=orecv_sem.at[me],
            device_id=(z, rr, cc, core), device_id_type=MESH)

    def o_wait(chip, b):
        pltpu.make_async_remote_copy(
            src_ref=obuf.at[0, 0],
            dst_ref=ob.at[b, :, pl.ds(pl.multiple_of(chip * pair, pair), pair)],
            send_sem=osend_sem.at[0, 0], recv_sem=orecv_sem.at[2 * chip + b],
            device_id=(z, r, c, k), device_id_type=MESH).wait_recv()

    def attend(i, _):
        rr, cc, chip = chip_from(i)
        q_wait(2 * chip)
        q_wait(2 * chip + 1)
        top = all_scores(chip, s0)
        out = finish(chip, s0, top)
        for core in range(2):
            obuf[i + 1, core] = out[core * tok:(core + 1) * tok]
            o_send(i + 1, core, rr, cc).start()
        return 0

    lax.fori_loop(0, n_step, attend, 0)
    q_wait(2 * my_chip + 1 - k)
    out = finish(my_chip, s0, all_scores(my_chip, s0))
    for core in range(2):
        obuf[0, core] = out[core * tok:(core + 1) * tok]
    o_send(0, 1 - k, r, c).start()
    ob[k, :, pl.ds(pl.multiple_of(my_chip * pair, pair), pair)] = obuf[0, k]

    wo_copy.wait()

    def o_arrive(i, _):
        _, _, chip = chip_to(i)
        o_wait(chip, 0)
        o_wait(chip, 1)
        return 0

    lax.fori_loop(0, n_step, o_arrive, 0)
    o_wait(my_chip, 1 - k)

    blk = 512

    def out_step(n, _):
        cs = pl.ds(pl.multiple_of(n * blk, blk), blk)
        y = lax.dot_general(ob[...].reshape(2 * tok, ch), wobuf[:, cs], NN, preferred_element_type=F32)
        y_ref[:, cs] = y.astype(BF16)
        return 0

    lax.fori_loop(0, ch // blk, out_step, 0)

    def drain(i, _):
        rr, cc, _ = chip_to(i)
        fr, fc, _ = chip_from(i)
        for b in range(2):
            kv_send(i + 1, b, rr, cc).wait_send()
            q_send(i + 1, b, rr, cc).wait_send()
            o_send(i + 1, b, fr, fc).wait_send()
        return 0

    lax.fori_loop(0, n_step, drain, 0)
    kv_send(0, 1 - k, r, c).wait_send()
    q_send(0, 1 - k, r, c).wait_send()
    o_send(0, 1 - k, r, c).wait_send()


def solution(mesh):
    tok_spec = P("data", ("row", "col", "core"), None)
    rows, cols, cores = mesh.shape["row"], mesh.shape["col"], mesh.shape["core"]

    def per_device(tokens, w_qkv, w_out):
        batch, tok, ch = tokens.shape
        _, _, heads, head = w_qkv.shape
        chips = rows * cols
        pair = heads // chips * head
        dims = (rows, cols, tok, pair, head)
        devs = chips * cores
        keys = devs * tok
        wt = jnp.transpose(w_qkv, (1, 2, 3, 0)).reshape(3 * heads * head, ch)
        wo = w_out.reshape(heads * head, ch)
        dma = pltpu.SemaphoreType.DMA
        y = pl.pallas_call(
            functools.partial(kernel, dims),
            out_shape=jax.ShapeDtypeStruct((batch * tok, ch), BF16),
            in_specs=[
                pl.BlockSpec(memory_space=pltpu.VMEM),
                pl.BlockSpec(memory_space=pl.ANY),
                pl.BlockSpec(memory_space=pl.ANY),
            ],
            out_specs=pl.BlockSpec(memory_space=pltpu.VMEM),
            scratch_shapes=[
                pltpu.VMEM((chips, 3, pair, ch), BF16),
                pltpu.VMEM((heads * head, ch), BF16),
                pltpu.VMEM((chips, 2, 3, tok, pair), BF16),
                pltpu.VMEM((2, devs, tok, pair), BF16),
                pltpu.VMEM((devs, tok, pair), BF16),
                pltpu.VMEM((pair, keys), BF16),
                pltpu.VMEM((keys, 4 * tok), F32),
                pltpu.VMEM((keys, 4 * tok), F32),
                pltpu.VMEM((chips, 2, tok, pair), BF16),
                pltpu.VMEM((2, tok, heads * head), BF16),
                dma((3, chips)),
                dma,
                dma((2, chips, 2)),
                dma((2, devs)),
                dma((chips, 2)),
                dma((devs,)),
            ],
            compiler_params=pltpu.CompilerParams(
                collective_id=0, has_side_effects=True, vmem_limit_bytes=60 * 1024 * 1024),
        )(tokens.reshape(batch * tok, ch), wt, wo)
        return y.reshape(batch, tok, ch)

    return jax.shard_map(per_device, mesh=mesh, in_specs=(tok_spec, P(), P()), out_specs=tok_spec, check_vma=False)
```

time: 213 us -> 56.6 us (0.27)
  matrix products: 72 us -> 0 us
  Pallas kernels: 0 us -> 54.5 us
  waiting for transfers between devices: 45.6 us -> 0 us
  blocking collectives: 40.7 us -> 0 us
  local copies, waits for them, and re-layouts: 32.4 us -> 1.88 us
  between operations: 13.5 us -> 0.01 us
  other arithmetic: 6.82 us -> 0 us
    dot_general x34 -> x0, matrix products: 72 us -> none  [the longest x16 25.8 us: key_step(): jnp.einsum('bhqk,bkhd->bhqd', weights.astype(jnp.bfloat16), kv_piece[:, :...]
    pallas_call x0 -> x1, Pallas kernels: none -> 54.5 us  [per_device(): pl.pallas_call(functools.partial(kernel, dims), out_shape=jax.ShapeDtypeS...]
    all_gather x1 -> x0, waiting for transfers between devices: 45.6 us -> none  [per_device(): kv_all = lax.all_gather(qkv_grp[:, :, 1:], 'row', axis=1, tiled=True)]
    all_to_all x2 -> x0, blocking collectives: 40.7 us -> none  [the longest x1 26.4 us: per_device(): qkv_grp = lax.all_to_all(qkv_loc, head_axes, 3, 1, tiled=True)]
    unnamed x8 -> x1, local copies, waits for them, and re-layouts: 15.2 us -> 1.88 us
    all_to_all x3 -> x0, local copies, waits for them, and re-layouts: 9.63 us -> none  [the longest x2 9.37 us: per_device(): qkv_grp = lax.all_to_all(qkv_loc, head_axes, 3, 1, tiled=True)]
    reduce_sum x16 -> x0, other arithmetic: 6.16 us -> none  [key_step(): run_sum = run_sum * rescale + jnp.sum(weights, axis=-1)]
    convert_element_type x1 -> x0, local copies, waits for them, and re-layouts: 4.57 us -> none  [per_device(): jnp.einsum('btc,cjhd->btjhd', tokens, w_qkv, preferred_element_type=jnp.f...]
  transfers between devices with their start and end apart: 1 -> 0, of which waited for: 1 -> 0; matrix products, arithmetic and copies ran while one was open for 1% -> 0% of each run, Pallas kernels for 0% -> 0%
where the time goes in v1:
time: 56.6 us; the launch traced here: 56.4 us
  Pallas kernels  54.5 us (96%)
  local copies, waits for them, and re-layouts  1.88 us (3%)
    pallas_call x1, Pallas kernels, per_device(): pl.pallas_call(functools.partial(kernel, dims), out_shape=jax.ShapeDtypeS...  54.5 us
    unnamed x1, local copies, waits for them, and re-layouts  1.88 us

profile of v1, /device:TPU:97, one launch (start us, length us, event | category | flops | bytes accessed | tf_op | source)
XLA Modules:
  0.0 56.4 jit_solution(14621167825893092151)
XLA Ops:
  0.0 54.5 %shard_map.37 = bf16[128,2048]{1,0:T(8,128)(2,1)} custom-call(bf16[128,2048]{1,0:T(8,128)(2,1)} %bitcast.9, bf16[6144,2048]{1,0:T(8,128)(2,1)} %bitcast.6, bf16[2048,2048]{1,0:T(8,128)(2,1)} %bitcast.7), custom_call_target="tpu_custom_call" | custom-call | tf_op jit(solution)/shard_map/pallas_call | solution.py:292
  54.5 1.9 %copy.5 = bf16[2,64,2048]{2,1,0:T(8,128)(2,1)} copy(bf16[2,64,2048]{2,1,0:T(8,128)(2,1)} %bitcast.8) | data formatting | bytes 1048576

commit v2 on v0

v2 whole, which is shorter than its diff:
```python
import functools

import jax
import jax.numpy as jnp
from jax import lax
from jax.experimental import pallas as pl
from jax.experimental.pallas import tpu as pltpu
from jax.sharding import PartitionSpec as P

MESH = pl.DeviceIdType.MESH
F32 = jnp.float32
BF16 = jnp.bfloat16
NT = (((1,), (1,)), ((), ()))
NN = (((1,), (0,)), ((), ()))
KEY_CHUNK = 512
WIDE = 3
UNIT = 2


def groups_of(n_step):
    sizes = [1, WIDE - 1] + [WIDE] * (n_step // WIDE - 1)
    starts = [sum(sizes[:g]) for g in range(len(sizes))]
    return list(zip(starts, sizes))


def hop_order(rows, cols):
    def hops(d, n):
        return min(d, n - d)

    offs = [(dy, dx) for dy in range(rows) for dx in range(cols)][1:]
    like = [[(2, 2)], [(1, 1), (3, 3)], [(2, 1), (2, 3), (0, 2)], [(1, 2), (3, 2), (2, 0)], [(1, 3), (3, 1), (0, 1)]]
    first = [o for group in like for o in group if o in offs]
    rest = [o for o in offs if o not in first]
    return first + sorted(rest, key=lambda o: -hops(o[0], rows) - hops(o[1], cols))


def pack_table(values, base):
    words = []
    for start in range(0, len(values), 8):
        words.append(sum(v * base**i for i, v in enumerate(values[start : start + 8])))
    return words


def kernel(dims, x_hbm, wt_hbm, wo_hbm, y_hbm, x_ref, wbuf, wqbuf, wobuf, sbuf, k_all, v_all, q_all, vt, s0, s1, obuf, ob, y_ref,
           x_sem, w_sem, wq_sem, wo_sem, send_sem, kv_sem, q_sem, o_sem, y_sem):
    rows, cols, tok, pair, head = dims
    chips = rows * cols
    ch = x_ref.shape[1]
    z = lax.axis_index("data")
    r = lax.axis_index("row")
    c = lax.axis_index("col")
    k = lax.axis_index("core")
    my_chip = r * cols + c
    order = hop_order(rows, cols)
    n_step = len(order)
    groups = groups_of(n_step)
    n_group = len(groups)
    own = 0
    dy_words = pack_table([o[0] for o in order], rows)
    dx_words = pack_table([o[1] for o in order], cols)

    def digit(words, base, i):
        val = words[0]
        for w, word in enumerate(words[1:]):
            val = val + (word - words[w]) * (jnp.minimum(i // (8 * (w + 1)), 1))
        shift = base.bit_length() - 1
        return lax.rem(lax.shift_right_logical(jnp.int32(0) + val, shift * lax.rem(i, 8)), base)

    def step_offset(i):
        if isinstance(i, int):
            return order[i]
        return digit(dy_words, rows, i), digit(dx_words, cols, i)

    def chip_to(i):
        dy, dx = step_offset(i)
        return lax.rem(r + dy, rows), lax.rem(c + dx, cols)

    def chip_from(i):
        dy, dx = step_offset(i)
        return lax.rem(r + rows - dy, rows), lax.rem(c + cols - dx, cols)

    x_copy = pltpu.make_async_copy(x_hbm, x_ref, x_sem)
    x_copy.start()

    def kv_weights(slot, chip, sem):
        for n in range(2):
            pltpu.make_async_copy(wt_hbm.at[(n + 1) * chips + chip], wbuf.at[2 * slot + n], sem).start()

    def q_weights(slot, chip, sem):
        pltpu.make_async_copy(wt_hbm.at[chip], wqbuf.at[slot], sem).start()

    def chip_id(i):
        rr, cc = chip_to(i)
        return rr * cols + cc

    n_q = n_step // WIDE

    def load_kv(g):
        start, count = groups[g]
        for i in range(start, start + count):
            kv_weights(i + 1, chip_id(i), w_sem.at[g])

    def load_q(g):
        for n in range(WIDE):
            i = g * WIDE + n
            q_weights(i + 1, chip_id(i), wq_sem.at[g])

    def loaded(ref, slot, count, sem):
        part = ref.at[pl.ds(slot, count)]
        pltpu.make_async_copy(part, part, sem).wait()

    load_kv(0)
    barrier = pltpu.get_barrier_semaphore()
    for i in range(n_step):
        rr, cc = chip_to(i)
        for core in range(2):
            pl.semaphore_signal(barrier, inc=1, device_id=(z, rr, cc, core), device_id_type=MESH)
    pl.semaphore_signal(barrier, inc=1, device_id=(z, r, c, 1 - k), device_id_type=MESH)

    load_kv(1)

    def project(w):
        return lax.dot_general(w, x_ref[...], NT, preferred_element_type=F32).astype(BF16).T

    def keep(val, piece, slot, n):
        for b in range(2):
            sbuf[piece, slot, b] = val[b * tok:(b + 1) * tok, n * pair:(n + 1) * pair]

    def project_kv(slot, count):
        val = project(wbuf[pl.ds(2 * slot, 2 * count)].reshape(2 * count * pair, ch))
        for n in range(2 * count):
            keep(val, n % 2, slot + n // 2, n)

    def project_q(slot, count):
        val = project(wqbuf[pl.ds(slot, count)].reshape(count * pair, ch))
        for n in range(count):
            keep(val, 2, slot + n, n)

    def remote(src, dst, sem_s, sem_r, rr, cc, core):
        return pltpu.make_async_remote_copy(
            src_ref=src, dst_ref=dst, send_sem=sem_s, recv_sem=sem_r,
            device_id=(z, rr, cc, core), device_id_type=MESH)

    def kv_send(i, g):
        rr, cc = chip_to(i)
        for b in range(2):
            for n, dst in ((0, k_all), (1, v_all)):
                remote(sbuf.at[n, i + 1, b], dst.at[i + 1, k], send_sem.at[0], kv_sem.at[g], rr, cc, b).start()

    def q_send(i):
        rr, cc = chip_to(i)
        for b in range(2):
            remote(sbuf.at[2, i + 1, b], q_all.at[i + 1, k], send_sem.at[0], q_sem.at[(i + 1) // 2], rr, cc, b).start()

    def kv_group(g, start, count):
        loaded(wbuf, 2 * (start + 1), 2 * count, w_sem.at[g])
        project_kv(start + 1, count)

    def kv_group_send(g, start, count):
        for n in range(count):
            kv_send(start + n, g)

    x_copy.wait()
    load_kv(2)
    kv_group(0, *groups[0])
    for g in range(3, n_group):
        load_kv(g)
    with jax.named_scope("barrier"):
        pl.semaphore_wait(barrier, 2 * n_step + 1)
    kv_group_send(0, *groups[0])
    kv_group(1, *groups[1])
    kv_group_send(1, *groups[1])

    def kv_loop(g, _):
        load_q(g - 2)
        start = (g - 2) * WIDE + groups[2][0]
        kv_group(g, start, WIDE)
        kv_group_send(g, start, WIDE)
        return 0

    with jax.named_scope("kv_loop"):
        lax.fori_loop(2, n_group, kv_loop, 0)

    for g in range(n_group - 2, n_q):
        load_q(g)
    kv_weights(own, my_chip, w_sem.at[n_group])
    q_weights(own, my_chip, w_sem.at[n_group])

    def q_loop(g, _):
        start = g * WIDE
        loaded(wqbuf, start + 1, WIDE, wq_sem.at[g])
        project_q(start + 1, WIDE)
        return 0

    with jax.named_scope("q_loop"):
        lax.fori_loop(0, n_q, q_loop, 0)

    def flip(slot):
        val = v_all[slot].reshape(2 * tok, pair)
        vt[:, slot * 2 * tok:(slot + 1) * 2 * tok] = val.T

    def kv_arrive(g):
        start, count = groups[g]
        part = sbuf.at[pl.ds(0, 2), pl.ds(start + 1, count)]
        pltpu.make_async_copy(part, part, kv_sem.at[g]).wait()
        for i in range(start, start + count):
            q_send(i)
        for i in range(start, start + count):
            flip(i + 1)

    kv_arrive(0)
    kv_arrive(1)

    with jax.named_scope("own"):
        pltpu.make_async_copy(wo_hbm.at[my_chip], wobuf.at[own], wo_sem).start()
        for i in range(n_step):
            pltpu.make_async_copy(wo_hbm.at[chip_id(i)], wobuf.at[i + 1], wo_sem).start()
        loaded(wbuf, 2 * own, 2, w_sem.at[n_group])
        loaded(wqbuf, own, 1, w_sem.at[n_group])
        project_kv(own, 1)
        project_q(own, 1)
        for n, dst in ((0, k_all), (1, v_all), (2, q_all)):
            dst[own, k] = sbuf[n, own, k]
            remote(sbuf.at[n, own, 1 - k], dst.at[own, k], send_sem.at[1], kv_sem.at[n_group], r, c, 1 - k).start()

    with jax.named_scope("kv_arrive"):
        for g in range(2, n_group):
            kv_arrive(g)
        part = sbuf.at[:, 0, 0]
        pltpu.make_async_copy(part, part, kv_sem.at[n_group]).wait()
        flip(own)

    def arrived(ref, slot, count, sem):
        part = ref.at[pl.ds(slot, count)]
        pltpu.make_async_copy(part, part, sem).wait()

    keys = chips * 2 * tok
    lanes = 4 * tok * UNIT
    n_unit = chips // UNIT

    def queries(unit):
        parts = []
        for u in range(UNIT):
            q = q_all[unit * UNIT + u].reshape(2 * tok, pair) * BF16(head**-0.5)
            first = lax.broadcasted_iota(jnp.int32, q.shape, 1) < head
            zero = jnp.zeros_like(q)
            parts += [jnp.where(first, q, zero), jnp.where(first, zero, q)]
        return jnp.concatenate(parts, axis=0)

    def scores(qq, scr, lo, n):
        keys_c = k_all[lo // (2 * tok):(lo + n) // (2 * tok)].reshape(n, pair)
        s = lax.dot_general(keys_c, qq, NT, preferred_element_type=F32)
        scr[lo:lo + n] = s
        return jnp.max(s.reshape(n // 8, 8, lanes), axis=0)

    def weigh(scr, top, lo, n):
        w = jnp.exp(scr[lo:lo + n] - top)
        part = jnp.sum(w.reshape(n // 8, 8, lanes), axis=0)
        return part, lax.dot_general(vt[:, lo:lo + n], w.astype(BF16), NN, preferred_element_type=F32)

    def both(scr, top, next_unit, next_scr):
        new_top = total = acc = None
        qq = None if next_unit is None else queries(next_unit)
        for at in range(0, keys, KEY_CHUNK):
            if qq is not None:
                high = scores(qq, next_scr, at, KEY_CHUNK)
                new_top = high if new_top is None else jnp.maximum(new_top, high)
            if scr is not None:
                part, piece = weigh(scr, top, at, KEY_CHUNK)
                total = part if total is None else total + part
                acc = piece if acc is None else acc + piece
        if qq is not None:
            new_top = jnp.max(new_top, axis=0, keepdims=True)
        outs = []
        if scr is not None:
            total = jnp.sum(total, axis=0, keepdims=True)
            wide = 2 * tok
            for u in range(UNIT):
                a, b, e = 2 * u * wide, (2 * u + 1) * wide, (2 * u + 2) * wide
                out = jnp.concatenate([acc[:head, a:b] / total[:, a:b], acc[head:, b:e] / total[:, b:e]], axis=0)
                outs.append(out.T.astype(BF16))
        return outs, new_top

    half_slots = chips // 2

    def put(slot, out):
        rr, cc = chip_from(slot - 1)
        for core in range(2):
            obuf[slot, core] = out[core * tok:(core + 1) * tok]
            remote(obuf.at[slot, core], ob.at[k, :, pl.ds(pl.multiple_of(slot * pair, pair), pair)],
                   send_sem.at[2], o_sem.at[slot // half_slots], rr, cc, core).start()

    def put_own(out):
        for core in range(2):
            obuf[own, core] = out[core * tok:(core + 1) * tok]
        at = pl.ds(own * pair, pair)
        ob[k, :, at] = obuf[own, k]
        remote(obuf.at[own, 1 - k], ob.at[k, :, at], send_sem.at[3], o_sem.at[2], r, c, 1 - k).start()

    def q_wait(unit):
        with jax.named_scope("q_wait"):
            arrived(q_all, 1, UNIT, q_sem.at[unit])

    def attend(j, top):
        unit = 2 * j + 1
        for scr, next_scr in ((s1, s0), (s0, s1)):
            q_wait(unit + 1)
            outs, top = both(scr, top, unit + 1, next_scr)
            for u in range(UNIT):
                put(unit * UNIT + u, outs[u])
            unit = unit + 1
        return top

    with jax.named_scope("q_first"):
        arrived(q_all, 1, 1, q_sem.at[0])
    _, top = both(None, None, 0, s0)
    q_wait(1)
    outs, top = both(s0, top, 1, s1)
    put_own(outs[0])
    put(1, outs[1])
    with jax.named_scope("attend"):
        top = lax.fori_loop(0, (n_unit - 2) // 2, attend, top)
    with jax.named_scope("last"):
        outs, _ = both(s1, top, None, None)
        for u in range(UNIT):
            put((n_unit - 1) * UNIT + u, outs[u])

    blk = 512

    def o_part(lo, hi, n):
        cs = pl.ds(pl.multiple_of(n * blk, blk), blk)
        lhs = ob[:, :, lo:hi].reshape(2 * tok, hi - lo)
        w = wobuf[lo // pair:hi // pair, :, cs].reshape(hi - lo, blk)
        return lax.dot_general(lhs, w, NN, preferred_element_type=F32), cs

    cut = half_slots * pair

    def o_first(n, _):
        y, cs = o_part(0, cut, n)
        s0[pl.ds(pl.multiple_of(n * 2 * tok, 2 * tok), 2 * tok), :] = y
        return 0

    def o_second(n, _):
        y, cs = o_part(cut, ch, n)
        at = pl.ds(pl.multiple_of(n * 2 * tok, 2 * tok), 2 * tok)
        y = y + s0[at, :]
        y_ref[:, cs] = y.astype(BF16)
        pltpu.make_async_copy(y_ref.at[:, cs], y_hbm.at[:, cs], y_sem).start()
        return 0

    with jax.named_scope("o_arrive1"):
        pltpu.make_async_copy(wo_hbm, wobuf, wo_sem).wait()
        pltpu.make_async_copy(obuf.at[0, 0], obuf.at[0, 0], o_sem.at[2]).wait()
        arrived(obuf, 1, half_slots - 1, o_sem.at[0])
    with jax.named_scope("o_first"):
        lax.fori_loop(0, ch // blk, o_first, 0)
    with jax.named_scope("o_arrive2"):
        arrived(obuf, half_slots, chips - half_slots, o_sem.at[1])
    with jax.named_scope("o_second"):
        lax.fori_loop(0, ch // blk, o_second, 0)

    with jax.named_scope("drain"):
        rest = sbuf.at[:, pl.ds(1, n_step)]
        pltpu.make_async_copy(rest, rest, send_sem.at[0]).wait()
        pltpu.make_async_copy(sbuf.at[:, 0, 0], sbuf.at[:, 0, 0], send_sem.at[1]).wait()
        arrived(obuf, 1, n_step, send_sem.at[2])
        pltpu.make_async_copy(obuf.at[0, 0], obuf.at[0, 0], send_sem.at[3]).wait()
        pltpu.make_async_copy(y_ref, y_hbm, y_sem).wait()


def solution(mesh):
    tok_spec = P("data", ("row", "col", "core"), None)
    rows, cols, cores = mesh.shape["row"], mesh.shape["col"], mesh.shape["core"]

    def per_device(tokens, w_qkv, w_out):
        batch, tok, ch = tokens.shape
        _, _, heads, head = w_qkv.shape
        chips = rows * cols
        pair = heads // chips * head
        dims = (rows, cols, tok, pair, head)
        keys = chips * cores * tok
        wt = jnp.transpose(w_qkv, (1, 2, 3, 0)).reshape(3 * chips, pair, ch)
        wo = w_out.reshape(chips, pair, ch)
        dma = pltpu.SemaphoreType.DMA
        n_group = len(groups_of(chips - 1))
        y = pl.pallas_call(
            functools.partial(kernel, dims),
            out_shape=jax.ShapeDtypeStruct((batch * tok, ch), BF16),
            in_specs=[pl.BlockSpec(memory_space=pl.ANY)] * 3,
            out_specs=pl.BlockSpec(memory_space=pl.ANY),
            scratch_shapes=[
                pltpu.VMEM((batch * tok, ch), BF16),
                pltpu.VMEM((2 * chips, pair, ch), BF16),
                pltpu.VMEM((chips, pair, ch), BF16),
                pltpu.VMEM((chips, pair, ch), BF16),
                pltpu.VMEM((3, chips, 2, tok, pair), BF16),
                pltpu.VMEM((chips, 2, tok, pair), BF16),
                pltpu.VMEM((chips, 2, tok, pair), BF16),
                pltpu.VMEM((chips, 2, tok, pair), BF16),
                pltpu.VMEM((pair, keys), BF16),
                pltpu.VMEM((keys, 4 * tok * UNIT), F32),
                pltpu.VMEM((keys, 4 * tok * UNIT), F32),
                pltpu.VMEM((chips, 2, tok, pair), BF16),
                pltpu.VMEM((2, tok, heads * head), BF16),
                pltpu.VMEM((batch * tok, ch), BF16),
                dma,
                dma((n_group + 1,)),
                dma(((chips - 1) // WIDE,)),
                dma,
                dma((4,)),
                dma((n_group + 1,)),
                dma((chips // 2,)),
                dma((3,)),
                dma,
            ],
            compiler_params=pltpu.CompilerParams(
                collective_id=0, has_side_effects=True, vmem_limit_bytes=60 * 1024 * 1024),
        )(tokens.reshape(batch * tok, ch), wt, wo)
        return y.reshape(batch, tok, ch)

    return jax.shard_map(per_device, mesh=mesh, in_specs=(tok_spec, P(), P()), out_specs=tok_spec, check_vma=False)
```

time: 213 us -> 44.9 us (0.21)
  matrix products: 72 us -> 0 us
  waiting for transfers between devices: 45.6 us -> 0 us
  Pallas kernels: 0 us -> 42.9 us
  blocking collectives: 40.7 us -> 0 us
  local copies, waits for them, and re-layouts: 32.4 us -> 1.88 us
  between operations: 13.5 us -> 0.01 us
  other arithmetic: 6.82 us -> 0 us
    dot_general x34 -> x0, matrix products: 72 us -> none  [the longest x16 25.8 us: key_step(): jnp.einsum('bhqk,bkhd->bhqd', weights.astype(jnp.bfloat16), kv_piece[:, :...]
    all_gather x1 -> x0, waiting for transfers between devices: 45.6 us -> none  [per_device(): kv_all = lax.all_gather(qkv_grp[:, :, 1:], 'row', axis=1, tiled=True)]
    pallas_call x0 -> x1, Pallas kernels: none -> 42.9 us  [per_device(): pl.pallas_call(functools.partial(kernel, dims), out_shape=jax.ShapeDtypeS...]
    all_to_all x2 -> x0, blocking collectives: 40.7 us -> none  [the longest x1 26.4 us: per_device(): qkv_grp = lax.all_to_all(qkv_loc, head_axes, 3, 1, tiled=True)]
    unnamed x8 -> x1, local copies, waits for them, and re-layouts: 15.2 us -> 1.88 us
    all_to_all x3 -> x0, local copies, waits for them, and re-layouts: 9.63 us -> none  [the longest x2 9.37 us: per_device(): qkv_grp = lax.all_to_all(qkv_loc, head_axes, 3, 1, tiled=True)]
    reduce_sum x16 -> x0, other arithmetic: 6.16 us -> none  [key_step(): run_sum = run_sum * rescale + jnp.sum(weights, axis=-1)]
    convert_element_type x1 -> x0, local copies, waits for them, and re-layouts: 4.57 us -> none  [per_device(): jnp.einsum('btc,cjhd->btjhd', tokens, w_qkv, preferred_element_type=jnp.f...]
  transfers between devices with their start and end apart: 1 -> 0, of which waited for: 1 -> 0; matrix products, arithmetic and copies ran while one was open for 1% -> 0% of each run, Pallas kernels for 0% -> 0%
where the time goes in v2:
time: 44.9 us; the launch traced here: 44.8 us
  Pallas kernels  42.9 us (96%)
  local copies, waits for them, and re-layouts  1.88 us (4%)
    pallas_call x1, Pallas kernels, per_device(): pl.pallas_call(functools.partial(kernel, dims), out_shape=jax.ShapeDtypeS...  42.9 us
    unnamed x1, local copies, waits for them, and re-layouts  1.88 us

profile of v2, /device:TPU:97, one launch (start us, length us, event | category | flops | bytes accessed | tf_op | source)
XLA Modules:
  0.0 44.8 jit_solution(13529646925018219414)
XLA Ops:
  0.0 42.9 %shard_map.37 = bf16[128,2048]{1,0:T(8,128)(2,1)} custom-call(bf16[128,2048]{1,0:T(8,128)(2,1)} %bitcast.9, bf16[48,128,2048]{2,1,0:T(8,128)(2,1)} %bitcast.6, bf16[16,128,2048]{2,1,0:T(8,128)(2,1)} %bitcast.7), custom_call_target="tpu_custom_call" | custom-call | tf_op jit(solution)/shard_map/pallas_call | solution.py:386
  42.9 1.9 %copy.5 = bf16[2,64,2048]{2,1,0:T(8,128)(2,1)} copy(bf16[2,64,2048]{2,1,0:T(8,128)(2,1)} %bitcast.8) | data formatting | bytes 1048576

commit v3 on v2

--- a/solution.py
+++ b/solution.py
@@ -15,6 +15,7 @@
 KEY_CHUNK = 512
 WIDE = 3
 UNIT = 2
+BLOCK = 512
 
 
 def groups_of(n_step):
@@ -41,8 +42,8 @@
     return words
 
 
-def kernel(dims, x_hbm, wt_hbm, wo_hbm, y_hbm, x_ref, wbuf, wqbuf, wobuf, sbuf, k_all, v_all, q_all, vt, s0, s1, obuf, ob, y_ref,
-           x_sem, w_sem, wq_sem, wo_sem, send_sem, kv_sem, q_sem, o_sem, y_sem):
+def kernel(dims, x_hbm, wt_hbm, wo_hbm, ob, wobuf, y_part, x_ref, wbuf, wqbuf, sbuf, k_all, v_all, q_all, vt, s0, s1, obuf,
+           x_sem, w_sem, wq_sem, wo_sem, send_sem, kv_sem, q_sem, o_sem):
     rows, cols, tok, pair, head = dims
     chips = rows * cols
     ch = x_ref.shape[1]
@@ -325,27 +326,14 @@
         for u in range(UNIT):
             put((n_unit - 1) * UNIT + u, outs[u])
 
-    blk = 512
-
-    def o_part(lo, hi, n):
+    blk = BLOCK
+    cut = half_slots * pair
+
+    def o_first(n, _):
         cs = pl.ds(pl.multiple_of(n * blk, blk), blk)
-        lhs = ob[:, :, lo:hi].reshape(2 * tok, hi - lo)
-        w = wobuf[lo // pair:hi // pair, :, cs].reshape(hi - lo, blk)
-        return lax.dot_general(lhs, w, NN, preferred_element_type=F32), cs
-
-    cut = half_slots * pair
-
-    def o_first(n, _):
-        y, cs = o_part(0, cut, n)
-        s0[pl.ds(pl.multiple_of(n * 2 * tok, 2 * tok), 2 * tok), :] = y
-        return 0
-
-    def o_second(n, _):
-        y, cs = o_part(cut, ch, n)
-        at = pl.ds(pl.multiple_of(n * 2 * tok, 2 * tok), 2 * tok)
-        y = y + s0[at, :]
-        y_ref[:, cs] = y.astype(BF16)
-        pltpu.make_async_copy(y_ref.at[:, cs], y_hbm.at[:, cs], y_sem).start()
+        lhs = ob[:, :, :cut].reshape(2 * tok, cut)
+        w = wobuf[:half_slots, :, cs].reshape(cut, blk)
+        y_part[:, cs] = lax.dot_general(lhs, w, NN, preferred_element_type=F32)
         return 0
 
     with jax.named_scope("o_arrive1"):
@@ -354,18 +342,32 @@
         arrived(obuf, 1, half_slots - 1, o_sem.at[0])
     with jax.named_scope("o_first"):
         lax.fori_loop(0, ch // blk, o_first, 0)
-    with jax.named_scope("o_arrive2"):
-        arrived(obuf, half_slots, chips - half_slots, o_sem.at[1])
-    with jax.named_scope("o_second"):
-        lax.fori_loop(0, ch // blk, o_second, 0)
-
     with jax.named_scope("drain"):
         rest = sbuf.at[:, pl.ds(1, n_step)]
         pltpu.make_async_copy(rest, rest, send_sem.at[0]).wait()
         pltpu.make_async_copy(sbuf.at[:, 0, 0], sbuf.at[:, 0, 0], send_sem.at[1]).wait()
+        pltpu.make_async_copy(obuf.at[0, 0], obuf.at[0, 0], send_sem.at[3]).wait()
         arrived(obuf, 1, n_step, send_sem.at[2])
-        pltpu.make_async_copy(obuf.at[0, 0], obuf.at[0, 0], send_sem.at[3]).wait()
-        pltpu.make_async_copy(y_ref, y_hbm, y_sem).wait()
+    with jax.named_scope("o_arrive2"):
+        arrived(obuf, half_slots, chips - half_slots, o_sem.at[1])
+
+
+def finish_kernel(ob, wobuf, y_part, y_hbm, y_ref, y_sem):
+    _, tok, width = ob.shape
+    chips, pair, ch = wobuf.shape
+    half, cut = chips // 2, width // 2
+
+    def second(n, _):
+        cs = pl.ds(pl.multiple_of(n * BLOCK, BLOCK), BLOCK)
+        lhs = ob[:, :, cut:].reshape(2 * tok, width - cut)
+        w = wobuf[half:, :, cs].reshape(width - cut, BLOCK)
+        y = y_part[:, cs] + lax.dot_general(lhs, w, NN, preferred_element_type=F32)
+        y_ref[:, cs] = y.astype(BF16)
+        pltpu.make_async_copy(y_ref.at[:, cs], y_hbm.at[:, cs], y_sem).start()
+        return 0
+
+    lax.fori_loop(0, ch // BLOCK, second, 0)
+    pltpu.make_async_copy(y_ref, y_hbm, y_sem).wait()
 
 
 def solution(mesh):
@@ -383,15 +385,19 @@
         wo = w_out.reshape(chips, pair, ch)
         dma = pltpu.SemaphoreType.DMA
         n_group = len(groups_of(chips - 1))
-        y = pl.pallas_call(
+        vmem = pl.BlockSpec(memory_space=pltpu.VMEM)
+        ob, wobuf, y_part = pl.pallas_call(
             functools.partial(kernel, dims),
-            out_shape=jax.ShapeDtypeStruct((batch * tok, ch), BF16),
+            out_shape=(
+                pltpu.VMEM((2, tok, heads * head), BF16),
+                pltpu.VMEM((chips, pair, ch), BF16),
+                pltpu.VMEM((batch * tok, ch), F32),
+            ),
             in_specs=[pl.BlockSpec(memory_space=pl.ANY)] * 3,
-            out_specs=pl.BlockSpec(memory_space=pl.ANY),
+            out_specs=(vmem, vmem, vmem),
             scratch_shapes=[
                 pltpu.VMEM((batch * tok, ch), BF16),
                 pltpu.VMEM((2 * chips, pair, ch), BF16),
-                pltpu.VMEM((chips, pair, ch), BF16),
                 pltpu.VMEM((chips, pair, ch), BF16),
                 pltpu.VMEM((3, chips, 2, tok, pair), BF16),
                 pltpu.VMEM((chips, 2, tok, pair), BF16),
@@ -401,8 +407,6 @@
                 pltpu.VMEM((keys, 4 * tok * UNIT), F32),
                 pltpu.VMEM((keys, 4 * tok * UNIT), F32),
                 pltpu.VMEM((chips, 2, tok, pair), BF16),
-                pltpu.VMEM((2, tok, heads * head), BF16),
-                pltpu.VMEM((batch * tok, ch), BF16),
                 dma,
                 dma((n_group + 1,)),
                 dma(((chips - 1) // WIDE,)),
@@ -411,11 +415,18 @@
                 dma((n_group + 1,)),
                 dma((chips // 2,)),
                 dma((3,)),
-                dma,
             ],
             compiler_params=pltpu.CompilerParams(
-                collective_id=0, has_side_effects=True, vmem_limit_bytes=60 * 1024 * 1024),
+                collective_id=0, has_side_effects=True, vmem_limit_bytes=44 * 1024 * 1024),
         )(tokens.reshape(batch * tok, ch), wt, wo)
+        y = pl.pallas_call(
+            finish_kernel,
+            out_shape=jax.ShapeDtypeStruct((batch * tok, ch), BF16),
+            in_specs=[vmem] * 3,
+            out_specs=pl.BlockSpec(memory_space=pl.ANY),
+            scratch_shapes=[pltpu.VMEM((batch * tok, ch), BF16), dma],
+            compiler_params=pltpu.CompilerParams(vmem_limit_bytes=8 * 1024 * 1024),
+        )(ob, wobuf, y_part)
         return y.reshape(batch, tok, ch)
 
     return jax.shard_map(per_device, mesh=mesh, in_specs=(tok_spec, P(), P()), out_specs=tok_spec, check_vma=False)

time: 44.9 us -> 43 us (0.958)
  local copies, waits for them, and re-layouts: 1.88 us -> 0 us
    unnamed x1 -> x0, local copies, waits for them, and re-layouts: 1.88 us -> none
    pallas_call x1 -> x2, Pallas kernels: 42.9 us -> 42.9 us  [the longest x1 41 us: per_device(): pl.pallas_call(functools.partial(kernel, dims), out_shape=(pltpu.VMEM((2,...]
where the time goes in v3:
time: 43 us; the launch traced here: 42.9 us
  Pallas kernels  42.9 us (100%)
    pallas_call x1, Pallas kernels, per_device(): pl.pallas_call(functools.partial(kernel, dims), out_shape=(pltpu.VMEM((2,...  41 us
    pallas_call x1, Pallas kernels, per_device(): pl.pallas_call(finish_kernel, out_shape=jax.ShapeDtypeStruct((batch * tok...  1.95 us

profile of v3, /device:TPU:97, one launch (start us, length us, event | category | flops | bytes accessed | tf_op | source)
XLA Modules:
  0.0 42.9 jit_solution(188870707660170035)
XLA Ops:
  0.0 41.0 %shard_map.37 = (bf16[2,64,2048]{2,1,0:T(8,128)(2,1)S(1)}, bf16[16,128,2048]{2,1,0:T(8,128)(2,1)S(1)}, f32[128,2048]{1,0:T(8,128)S(1)}) custom-call(bf16[128,2048]{1,0:T(8,128)(2,1)} %bitcast.8, bf16[48,128,2048]{2,1,0:T(8,128)(2,1)} %bitcast.6, bf16[16,128,2048]{2,1,0:T(8,128)(2,1)} %bitcast.7), custom_call_target="tpu_custom_call" | custom-call | tf_op jit(solution)/shard_map/pallas_call | solution.py:389
  41.0 2.0 %shard_map.38 = bf16[128,2048]{1,0:T(8,128)(2,1)} custom-call(bf16[2,64,2048]{2,1,0:T(8,128)(2,1)S(1)} %get-tuple-element.8.ob, bf16[16,128,2048]{2,1,0:T(8,128)(2,1)S(1)} %get-tuple-element.9.wobuf, f32[128,2048]{1,0:T(8,128)S(1)} %get-tuple-element.10.y_part), custom_call_target="tpu_custom_call" | custom-call | tf_op jit(solution)/shard_map/pallas_call | solution.py:422

commit v4 on v3

--- a/solution.py
+++ b/solution.py
@@ -15,7 +15,7 @@
 KEY_CHUNK = 512
 WIDE = 3
 UNIT = 2
-BLOCK = 512
+BLOCK = 2048
 
 
 def groups_of(n_step):
@@ -33,6 +33,15 @@
     first = [o for group in like for o in group if o in offs]
     rest = [o for o in offs if o not in first]
     return first + sorted(rest, key=lambda o: -hops(o[0], rows) - hops(o[1], cols))
+
+
+def query_order(rows, cols):
+    def hops(d, n):
+        return min(d, n - d)
+
+    offs = [(dy, dx) for dy in range(rows) for dx in range(cols)][1:]
+    near, mid, far = ([o for o in offs if lo <= hops(o[0], rows) + hops(o[1], cols) <= hi] for lo, hi in ((1, 1), (2, 2), (3, 4)))
+    return near[:3] + mid[:2] + far + mid[2:] + near[3:]
 
 
 def pack_table(values, base):
@@ -53,31 +62,33 @@
     k = lax.axis_index("core")
     my_chip = r * cols + c
     order = hop_order(rows, cols)
+    q_order = query_order(rows, cols)
     n_step = len(order)
     groups = groups_of(n_step)
     n_group = len(groups)
     own = 0
-    dy_words = pack_table([o[0] for o in order], rows)
-    dx_words = pack_table([o[1] for o in order], cols)
-
-    def digit(words, base, i):
-        val = words[0]
-        for w, word in enumerate(words[1:]):
-            val = val + (word - words[w]) * (jnp.minimum(i // (8 * (w + 1)), 1))
+    q_own = n_step
+    words = {id(o): (pack_table([d[0] for d in o], rows), pack_table([d[1] for d in o], cols)) for o in (order, q_order)}
+
+    def digit(table, base, i):
+        val = table[0]
+        for w, word in enumerate(table[1:]):
+            val = val + (word - table[w]) * (jnp.minimum(i // (8 * (w + 1)), 1))
         shift = base.bit_length() - 1
         return lax.rem(lax.shift_right_logical(jnp.int32(0) + val, shift * lax.rem(i, 8)), base)
 
-    def step_offset(i):
+    def offset(i, table):
         if isinstance(i, int):
-            return order[i]
+            return table[i]
+        dy_words, dx_words = words[id(table)]
         return digit(dy_words, rows, i), digit(dx_words, cols, i)
 
-    def chip_to(i):
-        dy, dx = step_offset(i)
+    def chip_to(i, table=order):
+        dy, dx = offset(i, table)
         return lax.rem(r + dy, rows), lax.rem(c + dx, cols)
 
-    def chip_from(i):
-        dy, dx = step_offset(i)
+    def chip_from(i, table=order):
+        dy, dx = offset(i, table)
         return lax.rem(r + rows - dy, rows), lax.rem(c + cols - dx, cols)
 
     x_copy = pltpu.make_async_copy(x_hbm, x_ref, x_sem)
@@ -90,8 +101,8 @@
     def q_weights(slot, chip, sem):
         pltpu.make_async_copy(wt_hbm.at[chip], wqbuf.at[slot], sem).start()
 
-    def chip_id(i):
-        rr, cc = chip_to(i)
+    def chip_id(i, table=order):
+        rr, cc = chip_to(i, table)
         return rr * cols + cc
 
     n_q = n_step // WIDE
@@ -104,7 +115,7 @@
     def load_q(g):
         for n in range(WIDE):
             i = g * WIDE + n
-            q_weights(i + 1, chip_id(i), wq_sem.at[g])
+            q_weights(i, chip_id(i, q_order), wq_sem.at[g])
 
     def loaded(ref, slot, count, sem):
         part = ref.at[pl.ds(slot, count)]
@@ -149,9 +160,9 @@
                 remote(sbuf.at[n, i + 1, b], dst.at[i + 1, k], send_sem.at[0], kv_sem.at[g], rr, cc, b).start()
 
     def q_send(i):
-        rr, cc = chip_to(i)
+        rr, cc = chip_to(i, q_order)
         for b in range(2):
-            remote(sbuf.at[2, i + 1, b], q_all.at[i + 1, k], send_sem.at[0], q_sem.at[(i + 1) // 2], rr, cc, b).start()
+            remote(sbuf.at[2, i, b], q_all.at[i, k], send_sem.at[0], q_sem.at[i // UNIT], rr, cc, b).start()
 
     def kv_group(g, start, count):
         loaded(wbuf, 2 * (start + 1), 2 * count, w_sem.at[g])
@@ -185,12 +196,12 @@
     for g in range(n_group - 2, n_q):
         load_q(g)
     kv_weights(own, my_chip, w_sem.at[n_group])
-    q_weights(own, my_chip, w_sem.at[n_group])
+    q_weights(q_own, my_chip, w_sem.at[n_group])
 
     def q_loop(g, _):
         start = g * WIDE
-        loaded(wqbuf, start + 1, WIDE, wq_sem.at[g])
-        project_q(start + 1, WIDE)
+        loaded(wqbuf, start, WIDE, wq_sem.at[g])
+        project_q(start, WIDE)
         return 0
 
     with jax.named_scope("q_loop"):
@@ -213,16 +224,16 @@
     kv_arrive(1)
 
     with jax.named_scope("own"):
-        pltpu.make_async_copy(wo_hbm.at[my_chip], wobuf.at[own], wo_sem).start()
         for i in range(n_step):
-            pltpu.make_async_copy(wo_hbm.at[chip_id(i)], wobuf.at[i + 1], wo_sem).start()
+            pltpu.make_async_copy(wo_hbm.at[chip_id(i, q_order)], wobuf.at[i], wo_sem).start()
+        pltpu.make_async_copy(wo_hbm.at[my_chip], wobuf.at[q_own], wo_sem).start()
         loaded(wbuf, 2 * own, 2, w_sem.at[n_group])
-        loaded(wqbuf, own, 1, w_sem.at[n_group])
+        loaded(wqbuf, q_own, 1, w_sem.at[n_group])
         project_kv(own, 1)
-        project_q(own, 1)
-        for n, dst in ((0, k_all), (1, v_all), (2, q_all)):
-            dst[own, k] = sbuf[n, own, k]
-            remote(sbuf.at[n, own, 1 - k], dst.at[own, k], send_sem.at[1], kv_sem.at[n_group], r, c, 1 - k).start()
+        project_q(q_own, 1)
+        for n, dst, at in ((0, k_all, own), (1, v_all, own), (2, q_all, q_own)):
+            dst[at, k] = sbuf[n, at, k]
+            remote(sbuf.at[n, at, 1 - k], dst.at[at, k], send_sem.at[1], kv_sem.at[n_group], r, c, 1 - k).start()
 
     with jax.named_scope("kv_arrive"):
         for g in range(2, n_group):
@@ -285,7 +296,7 @@
     half_slots = chips // 2
 
     def put(slot, out):
-        rr, cc = chip_from(slot - 1)
+        rr, cc = chip_from(slot, q_order)
         for core in range(2):
             obuf[slot, core] = out[core * tok:(core + 1) * tok]
             remote(obuf.at[slot, core], ob.at[k, :, pl.ds(pl.multiple_of(slot * pair, pair), pair)],
@@ -293,18 +304,18 @@
 
     def put_own(out):
         for core in range(2):
-            obuf[own, core] = out[core * tok:(core + 1) * tok]
-        at = pl.ds(own * pair, pair)
-        ob[k, :, at] = obuf[own, k]
-        remote(obuf.at[own, 1 - k], ob.at[k, :, at], send_sem.at[3], o_sem.at[2], r, c, 1 - k).start()
-
-    def q_wait(unit):
+            obuf[q_own, core] = out[core * tok:(core + 1) * tok]
+        at = pl.ds(q_own * pair, pair)
+        ob[k, :, at] = obuf[q_own, k]
+        remote(obuf.at[q_own, 1 - k], ob.at[k, :, at], send_sem.at[3], o_sem.at[2], r, c, 1 - k).start()
+
+    def q_wait(unit, count=UNIT):
         with jax.named_scope("q_wait"):
-            arrived(q_all, 1, UNIT, q_sem.at[unit])
+            arrived(q_all, 0, count, q_sem.at[unit])
 
     def attend(j, top):
-        unit = 2 * j + 1
-        for scr, next_scr in ((s1, s0), (s0, s1)):
+        unit = 2 * j
+        for scr, next_scr in ((s0, s1), (s1, s0)):
             q_wait(unit + 1)
             outs, top = both(scr, top, unit + 1, next_scr)
             for u in range(UNIT):
@@ -312,19 +323,18 @@
             unit = unit + 1
         return top
 
-    with jax.named_scope("q_first"):
-        arrived(q_all, 1, 1, q_sem.at[0])
+    q_wait(0)
     _, top = both(None, None, 0, s0)
-    q_wait(1)
-    outs, top = both(s0, top, 1, s1)
-    put_own(outs[0])
-    put(1, outs[1])
     with jax.named_scope("attend"):
         top = lax.fori_loop(0, (n_unit - 2) // 2, attend, top)
     with jax.named_scope("last"):
+        q_wait(n_unit - 1, UNIT - 1)
+        outs, top = both(s0, top, n_unit - 1, s1)
+        for u in range(UNIT):
+            put((n_unit - 2) * UNIT + u, outs[u])
         outs, _ = both(s1, top, None, None)
-        for u in range(UNIT):
-            put((n_unit - 1) * UNIT + u, outs[u])
+        put(q_own - 1, outs[0])
+        put_own(outs[1])
 
     blk = BLOCK
     cut = half_slots * pair
@@ -338,8 +348,7 @@
 
     with jax.named_scope("o_arrive1"):
         pltpu.make_async_copy(wo_hbm, wobuf, wo_sem).wait()
-        pltpu.make_async_copy(obuf.at[0, 0], obuf.at[0, 0], o_sem.at[2]).wait()
-        arrived(obuf, 1, half_slots - 1, o_sem.at[0])
+        arrived(obuf, 0, half_slots, o_sem.at[0])
     with jax.named_scope("o_first"):
         lax.fori_loop(0, ch // blk, o_first, 0)
     with jax.named_scope("drain"):
@@ -347,9 +356,10 @@
         pltpu.make_async_copy(rest, rest, send_sem.at[0]).wait()
         pltpu.make_async_copy(sbuf.at[:, 0, 0], sbuf.at[:, 0, 0], send_sem.at[1]).wait()
         pltpu.make_async_copy(obuf.at[0, 0], obuf.at[0, 0], send_sem.at[3]).wait()
-        arrived(obuf, 1, n_step, send_sem.at[2])
+        arrived(obuf, 0, n_step, send_sem.at[2])
     with jax.named_scope("o_arrive2"):
-        arrived(obuf, half_slots, chips - half_slots, o_sem.at[1])
+        arrived(obuf, half_slots, n_step - half_slots, o_sem.at[1])
+        pltpu.make_async_copy(obuf.at[0, 0], obuf.at[0, 0], o_sem.at[2]).wait()
 
 
 def finish_kernel(ob, wobuf, y_part, y_hbm, y_ref, y_sem):

time: 43 us -> 43.5 us (1.012)
  Pallas kernels: 42.9 us -> 43.4 us
    pallas_call x1, Pallas kernels: 41 us -> 41.9 us  [per_device(): pl.pallas_call(functools.partial(kernel, dims), out_shape=(pltpu.VMEM((2,...]
where the time goes in v4:
time: 43.5 us; the launch traced here: 43.4 us
  Pallas kernels  43.4 us (100%)
    pallas_call x1, Pallas kernels, per_device(): pl.pallas_call(functools.partial(kernel, dims), out_shape=(pltpu.VMEM((2,...  41.9 us
    pallas_call x1, Pallas kernels, per_device(): pl.pallas_call(finish_kernel, out_shape=jax.ShapeDtypeStruct((batch * tok...  1.53 us

profile of v4, /device:TPU:97, one launch (start us, length us, event | category | flops | bytes accessed | tf_op | source)
XLA Modules:
  0.0 43.4 jit_solution(17421340006102168785)
XLA Ops:
  0.0 41.9 %shard_map.37 = (bf16[2,64,2048]{2,1,0:T(8,128)(2,1)S(1)}, bf16[16,128,2048]{2,1,0:T(8,128)(2,1)S(1)}, f32[128,2048]{1,0:T(8,128)S(1)}) custom-call(bf16[128,2048]{1,0:T(8,128)(2,1)} %bitcast.8, bf16[48,128,2048]{2,1,0:T(8,128)(2,1)} %bitcast.6, bf16[16,128,2048]{2,1,0:T(8,128)(2,1)} %bitcast.7), custom_call_target="tpu_custom_call" | custom-call | tf_op jit(solution)/shard_map/pallas_call | solution.py:399
  41.9 1.5 %shard_map.38 = bf16[128,2048]{1,0:T(8,128)(2,1)} custom-call(bf16[2,64,2048]{2,1,0:T(8,128)(2,1)S(1)} %get-tuple-element.8.ob, bf16[16,128,2048]{2,1,0:T(8,128)(2,1)S(1)} %get-tuple-element.9.wobuf, f32[128,2048]{1,0:T(8,128)S(1)} %get-tuple-element.10.y_part), custom_call_target="tpu_custom_call" | custom-call | tf_op jit(solution)/shard_map/pallas_call | solution.py:432

commit v5 on v4

--- a/solution.py
+++ b/solution.py
@@ -41,7 +41,7 @@
 
     offs = [(dy, dx) for dy in range(rows) for dx in range(cols)][1:]
     near, mid, far = ([o for o in offs if lo <= hops(o[0], rows) + hops(o[1], cols) <= hi] for lo, hi in ((1, 1), (2, 2), (3, 4)))
-    return near[:3] + mid[:2] + far + mid[2:] + near[3:]
+    return near[:3] + mid + far + near[3:]
 
 
 def pack_table(values, base):
@@ -177,10 +177,10 @@
     kv_group(0, *groups[0])
     for g in range(3, n_group):
         load_kv(g)
+    kv_group(1, *groups[1])
     with jax.named_scope("barrier"):
         pl.semaphore_wait(barrier, 2 * n_step + 1)
     kv_group_send(0, *groups[0])
-    kv_group(1, *groups[1])
     kv_group_send(1, *groups[1])
 
     def kv_loop(g, _):

time: 43.5 us -> 41.6 us (0.956)
  Pallas kernels: 43.4 us -> 41.5 us
    pallas_call x1, Pallas kernels: 41.9 us -> 39.9 us  [per_device(): pl.pallas_call(functools.partial(kernel, dims), out_shape=(pltpu.VMEM((2,...]
where the time goes in v5:
time: 41.6 us; the launch traced here: 41.5 us
  Pallas kernels  41.5 us (100%)
    pallas_call x1, Pallas kernels, per_device(): pl.pallas_call(functools.partial(kernel, dims), out_shape=(pltpu.VMEM((2,...  39.9 us
    pallas_call x1, Pallas kernels, per_device(): pl.pallas_call(finish_kernel, out_shape=jax.ShapeDtypeStruct((batch * tok...  1.53 us

profile of v5, /device:TPU:97, one launch (start us, length us, event | category | flops | bytes accessed | tf_op | source)
XLA Modules:
  0.0 41.5 jit_solution(9580951238842224056)
XLA Ops:
  0.0 39.9 %shard_map.37 = (bf16[2,64,2048]{2,1,0:T(8,128)(2,1)S(1)}, bf16[16,128,2048]{2,1,0:T(8,128)(2,1)S(1)}, f32[128,2048]{1,0:T(8,128)S(1)}) custom-call(bf16[128,2048]{1,0:T(8,128)(2,1)} %bitcast.8, bf16[48,128,2048]{2,1,0:T(8,128)(2,1)} %bitcast.6, bf16[16,128,2048]{2,1,0:T(8,128)(2,1)} %bitcast.7), custom_call_target="tpu_custom_call" | custom-call | tf_op jit(solution)/shard_map/pallas_call | solution.py:399
  39.9 1.5 %shard_map.38 = bf16[128,2048]{1,0:T(8,128)(2,1)} custom-call(bf16[2,64,2048]{2,1,0:T(8,128)(2,1)S(1)} %get-tuple-element.8.ob, bf16[16,128,2048]{2,1,0:T(8,128)(2,1)S(1)} %get-tuple-element.9.wobuf, f32[128,2048]{1,0:T(8,128)S(1)} %get-tuple-element.10.y_part), custom_call_target="tpu_custom_call" | custom-call | tf_op jit(solution)/shard_map/pallas_call | solution.py:432

commit v6 on v5

--- a/solution.py
+++ b/solution.py
@@ -217,8 +217,9 @@
         pltpu.make_async_copy(part, part, kv_sem.at[g]).wait()
         for i in range(start, start + count):
             q_send(i)
-        for i in range(start, start + count):
-            flip(i + 1)
+        if g < n_group - 1:
+            for i in range(start, start + count):
+                flip(i + 1)
 
     kv_arrive(0)
     kv_arrive(1)
@@ -236,11 +237,12 @@
             remote(sbuf.at[n, at, 1 - k], dst.at[at, k], send_sem.at[1], kv_sem.at[n_group], r, c, 1 - k).start()
 
     with jax.named_scope("kv_arrive"):
-        for g in range(2, n_group):
+        for g in range(2, n_group - 1):
             kv_arrive(g)
         part = sbuf.at[:, 0, 0]
         pltpu.make_async_copy(part, part, kv_sem.at[n_group]).wait()
         flip(own)
+        kv_arrive(n_group - 1)
 
     def arrived(ref, slot, count, sem):
         part = ref.at[pl.ds(slot, count)]
@@ -325,6 +327,8 @@
 
     q_wait(0)
     _, top = both(None, None, 0, s0)
+    for i in range(groups[-1][0], sum(groups[-1])):
+        flip(i + 1)
     with jax.named_scope("attend"):
         top = lax.fori_loop(0, (n_unit - 2) // 2, attend, top)
     with jax.named_scope("last"):

time: 41.6 us -> 41.6 us (level)
  no operation moved by 1% of the time
where the time goes in v6:
time: 41.6 us; the launch traced here: 41.5 us
  Pallas kernels  41.5 us (100%)
    pallas_call x1, Pallas kernels, per_device(): pl.pallas_call(functools.partial(kernel, dims), out_shape=(pltpu.VMEM((2,...  40 us
    pallas_call x1, Pallas kernels, per_device(): pl.pallas_call(finish_kernel, out_shape=jax.ShapeDtypeStruct((batch * tok...  1.53 us

profile of v6, /device:TPU:97, one launch (start us, length us, event | category | flops | bytes accessed | tf_op | source)
XLA Modules:
  0.0 41.5 jit_solution(8217092247088687653)
XLA Ops:
  0.0 40.0 %shard_map.37 = (bf16[2,64,2048]{2,1,0:T(8,128)(2,1)S(1)}, bf16[16,128,2048]{2,1,0:T(8,128)(2,1)S(1)}, f32[128,2048]{1,0:T(8,128)S(1)}) custom-call(bf16[128,2048]{1,0:T(8,128)(2,1)} %bitcast.8, bf16[48,128,2048]{2,1,0:T(8,128)(2,1)} %bitcast.6, bf16[16,128,2048]{2,1,0:T(8,128)(2,1)} %bitcast.7), custom_call_target="tpu_custom_call" | custom-call | tf_op jit(solution)/shard_map/pallas_call | solution.py:403
  40.0 1.5 %shard_map.38 = bf16[128,2048]{1,0:T(8,128)(2,1)} custom-call(bf16[2,64,2048]{2,1,0:T(8,128)(2,1)S(1)} %get-tuple-element.8.ob, bf16[16,128,2048]{2,1,0:T(8,128)(2,1)S(1)} %get-tuple-element.9.wobuf, f32[128,2048]{1,0:T(8,128)S(1)} %get-tuple-element.10.y_part), custom_call_target="tpu_custom_call" | custom-call | tf_op jit(solution)/shard_map/pallas_call | solution.py:436
